TPU v7x, 16 devices: a 4x2x1 block of a 4x4x8 slice. The times are simulated.
16 devices in a mesh: data: 2 (over y, z), expert: 8 (over x, core).
Axes of the slice: x: 4, y: 2, z: 1, core: 2. Of those that a mesh axis runs over, the one named last changes fastest.
The devices are a block of a 4x4x8 slice.
Arguments:
- token_rows: bfloat16 [2048, 2048], P(('data', 'expert')), parts along dimension 0
- expert_ids: int32 [2048, 6], P(('data', 'expert')), parts along dimension 0
- gate_weights: float32 [2048, 6], P(('data', 'expert')), parts along dimension 0
- w_in: bfloat16 [64, 2048, 1408], P('expert')
- w_out: bfloat16 [64, 1408, 2048], P('expert')
Outputs:
- output: bfloat16 [2048, 2048], P(('data', 'expert')), parts along dimension 0
There are 2 independent parts. A program takes and returns all parts, laid end to end along the dimension named above; an argument that names none is the same for every part.
All inputs are finite; a program needn't handle non-finite values.
Results may differ from a plain program's by a relative error of at most 0.001.
Values are sent between devices in bfloat16 or wider.
A program may use at most 768 MiB of HBM per device.

v0:
```python
import jax
import jax.numpy as jnp
from jax import lax
from jax.sharding import PartitionSpec as P


def route_local(expert_ids, experts):
    ids_t = expert_ids.T
    onehot = (ids_t[:, :, None] == jnp.arange(experts, dtype=jnp.int32)).astype(jnp.int32)
    running = jnp.cumsum(onehot, axis=1)
    counts = running[:, -1, :]
    rank_local = jnp.sum(onehot * running, axis=2) - 1
    return ids_t, counts, rank_local


def solution(mesh):
    groups = mesh.shape["expert"]
    row_spec = P(("data", "expert"), None)
    weight_spec = P("expert", None, None)

    def device_step(token_rows, expert_ids, gate_weights, w_in, w_out):
        tokens, top_k = expert_ids.shape
        local_experts, model_dim = w_in.shape[0], w_in.shape[1]
        experts = local_experts * groups
        mean_load = tokens * top_k // experts
        send_cap = 7 * mean_load // 4
        capacity = groups * mean_load
        rows_total = experts * send_cap
        ids_t, counts, rank_local = route_local(expert_ids, experts)
        inclusive = counts
        shift = 1
        while shift < groups:
            pairs_list = [(source, source + shift) for source in range(groups - shift)]
            inclusive = inclusive + lax.ppermute(inclusive, "expert", pairs_list)
            shift = shift * 2
        before = inclusive - counts
        totals = lax.psum(counts, "expert")
        prior = jnp.cumsum(totals, axis=0) - totals
        within = jnp.cumsum(counts, axis=0) - counts
        slot = jnp.take_along_axis(prior + before, ids_t, axis=1) + rank_local
        keep = slot < capacity
        target = ids_t * send_cap + jnp.take_along_axis(within, ids_t, axis=1) + rank_local
        token_ids = jnp.broadcast_to(jnp.arange(tokens, dtype=jnp.int32), (top_k, tokens))
        source_row = jnp.full((rows_total,), tokens, jnp.int32).at[jnp.where(keep, target, rows_total).reshape(-1)].set(token_ids.reshape(-1), mode="drop")
        padded = jnp.concatenate([token_rows, jnp.zeros((1, model_dim), token_rows.dtype)], axis=0)
        outbound = jnp.take(padded, source_row, axis=0).reshape(experts, send_cap, model_dim)
        inbound = lax.all_to_all(outbound, "expert", 0, 0, tiled=True).reshape(groups, local_experts, send_cap, model_dim)
        pre_act = jnp.einsum("gesd,edf->gesf", inbound, w_in, preferred_element_type=jnp.float32)
        hidden = jax.nn.gelu(pre_act).astype(jnp.bfloat16)
        expert_out = jnp.einsum("gesf,efd->gesd", hidden, w_out, preferred_element_type=jnp.float32).astype(jnp.bfloat16)
        returned = lax.all_to_all(expert_out.reshape(experts, send_cap, model_dim), "expert", 0, 0, tiled=True).reshape(rows_total, model_dim)
        picked = jnp.take(returned, target, axis=0)
        weight = jnp.where(keep, gate_weights.T, 0.0)
        mixed = jnp.sum(weight[:, :, None] * picked.astype(jnp.float32), axis=0)
        return (token_rows.astype(jnp.float32) + mixed).astype(jnp.bfloat16)

    return jax.shard_map(device_step, mesh=mesh, in_specs=(row_spec, row_spec, row_spec, weight_spec, weight_spec), out_specs=row_spec, check_vma=False)
```

profile of v0, /device:TPU:112, one launch (start us, length us, event | category | flops | bytes accessed | tf_op | source)
XLA Modules:
  0.0 286.7 jit_solution(3162806627704736464)
XLA Ops:
  0.0 0.0 copy-start
  0.0 0.0 copy-start.1
  0.0 0.9 fusion.19
  0.9 0.4 reduce_window_sum.28
  1.3 1.7 collective-permute-start
  3.1 0.7 fusion.24
  3.8 1.0 select_reduce_fusion
  4.8 0.0 collective-permute-done
  4.8 5.8 %collective-permute-start.1 = (s32[6,64]{1,0:T(8,128)S(1)}, s32[6,64]{1,0:T(8,128)S(1)}, u32[]{:S(2)}, u32[]{:S(2)}) collective-permute-start(s32[6,64]{1,0:T(8,128)S(1)} %get-tuple-element.13), channel_id=1, source_target_pairs={{0,2},{1,3},{2,4},{3,5},{4,6},{5,7},{8,10},{9,11},{10,12},{11,13},... | collective-permute-start | bytes 4616 | tf_op jit(solution)/shard_map/ppermute | solution.py:34
  10.6 8.9 %psum.7 = s32[6,64]{1,0:T(8,128)S(1)} all-reduce(s32[6,64]{1,0:T(8,128)S(1)} %bitcast.81), channel_id=1, replica_groups=mesh['data'=2,'expert'=8] {'expert'}, use_global_device_ids=true, to_apply=%region_1.2 | all-reduce | flops 384 | bytes 3072 | tf_op jit(solution)/shard_map/psum | solution.py:37
  19.5 1.1 concatenate.3
  20.6 3.5 %gather_fusion.3 = s32[768]{0:T(1024)S(1)} fusion(s32[6,64]{1,0:T(8,128)S(1)} %get-tuple-element.12, s32[768]{0:T(1024)S(1)} %fusion.24), kind=kCustom, calls=%fused_computation.1.clone | custom fusion | bytes 12288 | tf_op jit(solution)/shard_map/jit(take_along_axis)/gather | solution.py:42
  24.1 0.0 collective-permute-done.1
  24.1 3.2 %collective-permute-start.2 = (s32[6,64]{1,0:T(8,128)S(1)}, s32[6,64]{1,0:T(8,128)S(1)}, u32[]{:S(2)}, u32[]{:S(2)}) collective-permute-start(s32[6,64]{1,0:T(8,128)S(1)} %add.74), channel_id=1, source_target_pairs={{0,4},{1,5},{2,6},{3,7},{8,12},{9,13},{10,14},{11,15}} | collective-permute-start | bytes 4616 | tf_op jit(solution)/shard_map/ppermute | solution.py:34
  27.4 0.0 copy-done
  27.4 1.3 collective-permute-done.2
  28.7 3.5 %gather_fusion.2 = s32[768]{0:T(1024)S(1)} fusion(s32[6,64]{1,0:T(8,128)S(1)} %subtract_add_fusion, s32[768]{0:T(1024)S(1)} %fusion.24), kind=kCustom, calls=%fused_computation.clone | custom fusion | bytes 12288 | tf_op jit(solution)/shard_map/jit(take_along_axis)/gather | solution.py:40
  32.2 0.0 copy-done.1
  32.3 3.4 %scatter_custom_fusion = s32[1344]{0:T(1024)S(1)} fusion(s32[768]{0:T(1024)S(1)} %fusion.28, s32[768]{0:T(1024)S(1)} %iota_bitcast_fusion, s32[]{:T(128)} %constant.44.clone.1), kind=kCustom, calls=%fused_computation.46 | custom fusion | bytes 5380 | tf_op jit(solution)/shard_map/scatter | solution.py:44
  35.7 0.1 broadcast_in_dim.50
  35.9 6.8 %gather_fusion = bf16[1344,2048]{1,0:T(8,128)(2,1)} fusion(bf16[129,2048]{1,0:T(8,128)(2,1)S(1)} %concatenate.3, s32[2048]{0:T(1024)S(1)} %pad_clamp_fusion), kind=kCustom, calls=%fused_computation.2 | custom fusion | bytes 11015424 | tf_op jit(solution)/shard_map/jit(_take)/gather | solution.py:46
  42.7 8.1 %gather.14 = bf16[64,21,2048]{2,1,0:T(8,128)(2,1)} reshape(bf16[1344,2048]{1,0:T(8,128)(2,1)} %gather_fusion) | data formatting | bytes 11010048 | tf_op jit(solution)/shard_map/jit(_take)/gather | solution.py:46
  50.9 3.4 %broadcast_select_fusion = bf16[64,21,2048]{2,1,0:T(8,128)(2,1)S(1)} fusion(bf16[64,21,2048]{2,1,0:T(8,128)(2,1)} %gather.14, pred[64,21]{1,0:T(8,128)(4,1)S(1)} %broadcast_in_dim.50), kind=kLoop, calls=%fused_computation.21 | loop fusion | flops 2752512 | bytes 11011392 | tf_op jit(solution)/shard_map/jit(_take)/select_n | solution.py:46
  54.3 77.1 %all_to_all.10 = bf16[64,21,2048]{2,1,0:T(8,128)(2,1)} all-to-all(bf16[64,21,2048]{2,1,0:T(8,128)(2,1)S(1)} %broadcast_select_fusion), channel_id=1, replica_groups=mesh['data'=2,'expert'=8] {'expert'}, dimensions={0} | all-to-all | bytes 11010048 | tf_op jit(solution)/shard_map/all_to_all | solution.py:47
  131.4 30.0 %fusion.11 = bf16[8,8,21,1408]{3,2,0,1:T(8,128)(2,1)} fusion(bf16[8,2048,1408]{2,1,0:T(8,128)(2,1)} %param.10, bf16[8,8,21,2048]{3,2,1,0:T(8,128)(2,1)} %bitcast.76), kind=kOutput, calls=%fused_computation.17 | convolution fusion | flops 7768104960 | bytes 55427072 | tf_op jit(solution)/shard_map/gesd,edf->gesf/dot_general | solution.py:48
  161.4 18.9 %convert_bitcast_fusion = bf16[8,8,21,2048]{3,2,0,1:T(8,128)(2,1)S(1)} fusion(bf16[8,8,21,1408]{3,2,0,1:T(8,128)(2,1)} %fusion.11, bf16[8,1408,2048]{2,1,0:T(8,128)(2,1)} %param.11), kind=kOutput, calls=%fused_computation.20 | convolution fusion | flops 7753826304 | bytes 55427072 | tf_op jit(solution)/shard_map/gesf,efd->gesd/dot_general | solution.py:50
  180.3 3.2 %copy.33 = bf16[8,8,21,2048]{3,1,0,2:T(8,128)(2,1)S(1)} copy(bf16[8,8,21,2048]{3,2,0,1:T(8,128)(2,1)S(1)} %convert_bitcast_fusion) | data formatting | bytes 11010048 | tf_op jit(solution)/shard_map/convert_element_type | solution.py:50
  183.5 5.7 %copy.13 = bf16[64,21,2048]{2,1,0:T(8,128)(2,1)} copy(bf16[64,21,2048]{2,0,1:T(8,128)(2,1)S(1)} %bitcast.74) | data formatting | bytes 11010048 | tf_op jit(solution)/shard_map/reshape | solution.py:51
  189.2 4.9 %all-to-all-start.1 = ((bf16[64,21,2048]{2,1,0:T(8,128)(2,1)}), bf16[64,21,2048]{2,1,0:T(8,128)(2,1)}, u32[]{:S(2)}, u32[]{:S(2)}) async-start(bf16[64,21,2048]{2,1,0:T(8,128)(2,1)} %copy.13), calls=%async_computation.1 | async-start | bytes 12582912 | tf_op jit(solution)/shard_map/all_to_all | solution.py:51
  194.1 71.9 %all-to-all-done.1 = bf16[64,21,2048]{2,1,0:T(8,128)(2,1)} async-done(((bf16[64,21,2048]{2,1,0:T(8,128)(2,1)}), bf16[64,21,2048]{2,1,0:T(8,128)(2,1)}, u32[]{:S(2)}, u32[]{:S(2)}) %all-to-all-start.1) | async-done | bytes 5505056 | tf_op jit(solution)/shard_map/all_to_all | solution.py:51
  266.0 8.2 %reshape.74 = bf16[1344,2048]{1,0:T(8,128)(2,1)} reshape(bf16[64,21,2048]{2,1,0:T(8,128)(2,1)} %all-to-all-done.1) | data formatting | bytes 11010048 | tf_op jit(solution)/shard_map/reshape | solution.py:51
  274.2 9.6 %gather_fusion.1 = bf16[768,2048]{1,0:T(8,128)(2,1)S(1)} fusion(bf16[1344,2048]{1,0:T(8,128)(2,1)} %reshape.74, s32[1024]{0:T(1024)S(1)} %pad_clamp_fusion.1), kind=kCustom, calls=%fused_computation.3 | custom fusion | bytes 6294528 | tf_op jit(solution)/shard_map/jit(_take)/gather | solution.py:52
  283.8 0.9 multiply_reduce_fusion
  284.7 2.0 add_convert_fusion
  (16 shorter events, 0.2 us)
Async XLA Ops:
  0.0 27.4 %copy-start = (s32[128,6]{0,1:T(8,128)S(1)}, s32[128,6]{0,1:T(8,128)}, u32[]{:S(2)}) copy-start(s32[128,6]{0,1:T(8,128)} %param.8) | copy-start | bytes 9220
  0.0 32.2 %copy-start.1 = (f32[128,6]{0,1:T(8,128)S(1)}, f32[128,6]{0,1:T(8,128)}, u32[]{:S(2)}) copy-start(f32[128,6]{0,1:T(8,128)} %param.9) | copy-start | bytes 9220
  1.3 3.5 %collective-permute-start = (s32[6,64]{1,0:T(8,128)S(1)}, s32[6,64]{1,0:T(8,128)S(1)}, u32[]{:S(2)}, u32[]{:S(2)}) collective-permute-start(s32[6,64]{1,0:T(8,128)S(1)} %bitcast.79), channel_id=1, source_target_pairs={{0,1},{1,2},{2,3},{3,4},{4,5},{5,6},{6,7},{8,9},{9,10},{10,11},{11... | collective-permute-start | bytes 4616 | tf_op jit(solution)/shard_map/ppermute | solution.py:34
  4.8 19.3 %collective-permute-start.1 = (s32[6,64]{1,0:T(8,128)S(1)}, s32[6,64]{1,0:T(8,128)S(1)}, u32[]{:S(2)}, u32[]{:S(2)}) collective-permute-start(s32[6,64]{1,0:T(8,128)S(1)} %get-tuple-element.13), channel_id=1, source_target_pairs={{0,2},{1,3},{2,4},{3,5},{4,6},{5,7},{8,10},{9,11},{10,12},{11,13},... | collective-permute-start | bytes 4616 | tf_op jit(solution)/shard_map/ppermute | solution.py:34
  24.1 4.5 %collective-permute-start.2 = (s32[6,64]{1,0:T(8,128)S(1)}, s32[6,64]{1,0:T(8,128)S(1)}, u32[]{:S(2)}, u32[]{:S(2)}) collective-permute-start(s32[6,64]{1,0:T(8,128)S(1)} %add.74), channel_id=1, source_target_pairs={{0,4},{1,5},{2,6},{3,7},{8,12},{9,13},{10,14},{11,15}} | collective-permute-start | bytes 4616 | tf_op jit(solution)/shard_map/ppermute | solution.py:34
  189.2 76.8 %all-to-all-start.1 = ((bf16[64,21,2048]{2,1,0:T(8,128)(2,1)}), bf16[64,21,2048]{2,1,0:T(8,128)(2,1)}, u32[]{:S(2)}, u32[]{:S(2)}) async-start(bf16[64,21,2048]{2,1,0:T(8,128)(2,1)} %copy.13), calls=%async_computation.1 | async-start | bytes 12582912 | tf_op jit(solution)/shard_map/all_to_all | solution.py:51
where the time goes:
time: 288 us; the launch traced here: 287 us
  blocking collectives  86 us (30%)
  waiting for transfers between devices  73.2 us (25%)
  local copies, waits for them, and re-layouts  53.3 us (19%)
  matrix products  48.9 us (17%)
  starting transfers between devices  15.6 us (5%)
  other arithmetic  9.38 us (3%)
    all_to_all x1, blocking collectives, device_step(): lax.all_to_all(outbound, 'expert', 0, 0, tiled=True)  77.1 us
    all_to_all x1, waiting for transfers between devices, device_step(): lax.all_to_all(expert_out.reshape(experts, send_cap, model_dim), 'expert'...  71.9 us
    dot_general x1, matrix products, device_step(): jnp.einsum('gesd,edf->gesf', inbound, w_in, preferred_element_type=jnp.fl...  30 us
    dot_general x1, matrix products, device_step(): jnp.einsum('gesf,efd->gesd', hidden, w_out, preferred_element_type=jnp.fl...  18.9 us
    gather x2, local copies, waits for them, and re-layouts, device_step(): jnp.take(padded, source_row, axis=0).reshape(experts, send_cap, model_dim)  15 us
    ppermute x3, starting transfers between devices, device_step(): inclusive = inclusive + lax.ppermute(inclusive, 'expert', pairs_list)  10.7 us
    gather x1, local copies, waits for them, and re-layouts, device_step(): picked = jnp.take(returned, target, axis=0)  9.6 us
    psum x1, blocking collectives, device_step(): totals = lax.psum(counts, 'expert')  8.92 us
  transfers between devices with their start and end apart: 4, of which 2 were waited for; matrix products, arithmetic and copies ran while one was open for 2% of the time, Pallas kernels for 0%

commit v1 on v0

v1 whole, which is shorter than its diff:
```python
import functools

import jax
import jax.numpy as jnp
from jax import lax
from jax.experimental import pallas as pl
from jax.experimental.pallas import tpu as pltpu
from jax.sharding import PartitionSpec as P

MESH = pl.DeviceIdType.MESH
F32 = jnp.float32
BF16 = jnp.bfloat16
AXIS = "expert"
LANES = 128
IN_BLOCKS = 4
IN_DEPTH = 1
OUT_COLS = 256
OUT_DEPTH = 3
BIG_BF16 = 3.3895313892515355e38

OWN_R, OWN_L, OWN_P, RELAY_R, RELAY_L, FWD_L, FWD_R, FWD_A, FWD_B = range(9)
PART, FAR_R, FAR_L, NEAR_R, NEAR_L, MIX_R, MIX_L = range(7)


def body(n, capacity, ids_ref, gate_ref, x_hbm, w_in, w_out, out_hbm,
         ids_all, gates_all, x_all, pick, packed, mix, xg, acc, hid, obuf,
         part_send, part_recv, total, far_recv, fin_recv, out_buf, win_buf, wout_buf,
         meta_ssem, meta_rsem, d_ssem, d_rsem, r_ssem, r_rsem, x_sem, win_sem, wout_sem, out_sem):
    top_k, tokens = ids_ref.shape
    local_e, model, hidden = w_in.shape
    chips = n // 2
    kc_n = model // IN_BLOCKS
    oc_n = model // OUT_COLS
    slots = local_e * capacity

    me = lax.axis_index(AXIS)
    core = lax.rem(me, 2)
    chip = me // 2
    buddy = me + 1 - 2 * core
    other = 1 - core
    c_right = lax.rem(chip + 1, chips)
    c_far = lax.rem(chip + 2, chips)
    c_left = lax.rem(chip + 3, chips)

    def dev(c, k):
        return 2 * c + k

    right = dev(c_right, core)
    left = dev(c_left, core)

    def win_copy(e, kc):
        slot = lax.rem(kc, IN_DEPTH) * local_e + e
        return pltpu.make_async_copy(
            w_in.at[e, pl.ds(kc * kc_n, kc_n), :], win_buf.at[slot], win_sem.at[slot])

    def wout_copy(e, oc):
        slot = lax.rem(oc, OUT_DEPTH) * local_e + e
        return pltpu.make_async_copy(
            w_out.at[e, :, pl.ds(oc * OUT_COLS, OUT_COLS)], wout_buf.at[slot], wout_sem.at[slot])

    def x_rows(kc, d):
        return x_all.at[kc, pl.ds(d * tokens, tokens), :]

    def x_half(kc, d, h):
        half = tokens // 2
        return x_all.at[kc, pl.ds(d * tokens + h * half, half), :]

    def x_copy(kc):
        return pltpu.make_async_copy(
            x_hbm.at[:, pl.ds(kc * kc_n, kc_n)], x_rows(kc, me), x_sem.at[kc])

    for kc in range(IN_BLOCKS):
        x_copy(kc).start()

    @pl.loop(0, IN_DEPTH)
    def _(kc):
        @pl.loop(0, local_e)
        def _(e):
            win_copy(e, kc).start()

    @pl.loop(0, OUT_DEPTH)
    def _(oc):
        @pl.loop(0, local_e)
        def _(e):
            wout_copy(e, oc).start()

    barrier = pltpu.get_barrier_semaphore()
    for d in range(1, n):
        pl.semaphore_signal(barrier, inc=1, device_id={AXIS: lax.rem(me + d, n)}, device_id_type=MESH)
    pl.semaphore_wait(barrier, n - 1)

    def meta_copies(d):
        to = lax.rem(me + d, n)
        return (
            pltpu.make_async_remote_copy(
                src_ref=ids_ref, dst_ref=ids_all.at[me], send_sem=meta_ssem.at[0, d], recv_sem=meta_rsem.at[0, d],
                device_id={AXIS: to}, device_id_type=MESH),
            pltpu.make_async_remote_copy(
                src_ref=gate_ref, dst_ref=gates_all.at[me], send_sem=meta_ssem.at[1, d], recv_sem=meta_rsem.at[1, d],
                device_id={AXIS: to}, device_id_type=MESH),
        )

    for d in range(1, n):
        for c in meta_copies(d):
            c.start()
    ids_all[me] = ids_ref[...]
    gates_all[me] = gate_ref[...]

    def dcopy(kind, kc, ref, to):
        return pltpu.make_async_remote_copy(
            src_ref=ref, dst_ref=ref, send_sem=d_ssem.at[kind, kc], recv_sem=d_rsem.at[kind, kc],
            device_id={AXIS: to}, device_id_type=MESH)

    far = dev(c_far, core)

    def d_sent(kind, kc):
        if kind == OWN_R:
            return dcopy(kind, kc, x_rows(kc, me), right)
        if kind == OWN_L:
            return dcopy(kind, kc, x_rows(kc, me), left)
        if kind == OWN_P:
            return dcopy(kind, kc, x_rows(kc, me), buddy)
        if kind == RELAY_R:
            return dcopy(kind, kc, x_half(kc, left, 0), right)
        if kind == RELAY_L:
            return dcopy(kind, kc, x_half(kc, right, 1), left)
        if kind == FWD_L:
            return dcopy(kind, kc, x_rows(kc, left), buddy)
        if kind == FWD_R:
            return dcopy(kind, kc, x_rows(kc, right), buddy)
        if kind == FWD_A:
            return dcopy(kind, kc, x_half(kc, far, 0), buddy)
        return dcopy(kind, kc, x_half(kc, far, 1), buddy)

    def d_got(kind, kc):
        if kind == OWN_R:
            ref = x_rows(kc, left)
        elif kind == OWN_L:
            ref = x_rows(kc, right)
        elif kind == OWN_P:
            ref = x_rows(kc, buddy)
        elif kind == RELAY_R:
            ref = x_half(kc, far, 0)
        elif kind == RELAY_L:
            ref = x_half(kc, far, 1)
        elif kind == FWD_L:
            ref = x_rows(kc, dev(c_left, other))
        elif kind == FWD_R:
            ref = x_rows(kc, dev(c_right, other))
        elif kind == FWD_A:
            ref = x_half(kc, dev(c_far, other), 0)
        else:
            ref = x_half(kc, dev(c_far, other), 1)
        return dcopy(kind, kc, ref, buddy)

    def send_own(kc):
        x_copy(kc).wait()
        for kind in (OWN_R, OWN_L, OWN_P):
            d_sent(kind, kc).start()

    def stage1(kc):
        d_got(OWN_R, kc).wait_recv()
        d_sent(RELAY_R, kc).start()
        d_sent(FWD_L, kc).start()
        d_got(OWN_L, kc).wait_recv()
        d_sent(RELAY_L, kc).start()
        d_sent(FWD_R, kc).start()

    def stage2(kc):
        d_got(RELAY_R, kc).wait_recv()
        d_sent(FWD_A, kc).start()
        d_got(RELAY_L, kc).wait_recv()
        d_sent(FWD_B, kc).start()

    def stage3(kc):
        for kind in (OWN_P, FWD_L, FWD_R, FWD_A, FWD_B):
            d_got(kind, kc).wait_recv()

    send_own(0)
    send_own(1)

    for d in range(1, n):
        for c in meta_copies(d):
            c.wait_recv()

    sub = lax.broadcasted_iota(jnp.int32, (local_e, tokens), 0) + me * local_e
    hit = {}
    for b in range(n):
        for j in range(top_k):
            hit[b, j] = jnp.where(ids_all[b, j:j + 1, :] == sub, 1.0, 0.0).astype(F32)
    hits = jnp.concatenate([hit[b, j] for b in range(n) for j in range(top_k)], axis=0).astype(BF16)
    t_from = lax.broadcasted_iota(jnp.int32, (tokens, tokens), 0)
    t_to = lax.broadcasted_iota(jnp.int32, (tokens, tokens), 1)
    earlier = jnp.where(t_from < t_to, 1.0, 0.0).astype(BF16)
    ones = jnp.full((tokens, tokens), 1.0, BF16)
    within = jnp.dot(hits, earlier, preferred_element_type=F32)
    sums = jnp.dot(hits, ones, preferred_element_type=F32)
    running = jnp.zeros((local_e, tokens), F32)
    rank = [jnp.zeros((local_e, tokens), F32) for _ in range(n)]
    for j in range(top_k):
        for b in range(n):
            at = (b * top_k + j) * local_e
            rank[b] = rank[b] + hit[b, j] * (running + within[at:at + local_e])
            running = running + sums[at:at + local_e]
    slot_row = lax.broadcasted_iota(jnp.int32, (capacity, tokens), 0).astype(F32)
    for b in range(n):
        has = jnp.zeros((local_e, tokens), F32)
        gate = jnp.zeros((local_e, tokens), F32)
        for j in range(top_k):
            has = has + hit[b, j]
            gate = gate + hit[b, j] * gates_all[b, j:j + 1, :]
        slot = jnp.where((has > 0.0) & (rank[b] < capacity), rank[b], -1.0)
        g1 = jnp.minimum(gate, BIG_BF16).astype(BF16).astype(F32)
        g2 = (gate - g1).astype(BF16).astype(F32)
        g3 = gate - g1 - g2
        packed[b] = jnp.concatenate([slot, g1, g2, g3], axis=0)
        for e in range(local_e):
            pick[e * capacity:(e + 1) * capacity, b * tokens:(b + 1) * tokens] = jnp.where(
                slot[e:e + 1, :] == slot_row, 1.0, 0.0).astype(BF16)

    stage1(0)
    if IN_BLOCKS > 2:
        send_own(2)

    lane = lax.broadcasted_iota(jnp.int32, (tokens, LANES), 1)

    @pl.loop(0, n)
    def _(b):
        row = pl.multiple_of((lax.rem(b, 2) * chips + b // 2) * tokens, tokens)
        cols = jnp.concatenate(
            [packed[b], jnp.zeros((LANES - 4 * local_e, tokens), F32)], axis=0).T
        for tile in range(slots // LANES):
            first = tile * LANES // capacity
            last = (tile * LANES + LANES - 1) // capacity
            col = lane + tile * LANES

            def per_lane(k):
                out = cols[:, k * local_e + first:k * local_e + first + 1]
                out = jnp.broadcast_to(out, (tokens, LANES))
                for e in range(first + 1, last + 1):
                    nxt = cols[:, k * local_e + e:k * local_e + e + 1]
                    out = jnp.where(col >= e * capacity, nxt, out)
                return out

            rel = col - first * capacity
            for e in range(first + 1, last + 1):
                rel = jnp.where(col >= e * capacity, col - e * capacity, rel)
            sel = per_lane(0) == rel.astype(F32)
            for k in range(3):
                mix[k, pl.ds(row, tokens), tile * LANES:(tile + 1) * LANES] = jnp.where(
                    sel, per_lane(k + 1), 0.0).astype(BF16)

    for kc in range(IN_BLOCKS):
        if kc + 1 < IN_BLOCKS:
            stage1(kc + 1)
            if kc + 3 < IN_BLOCKS:
                send_own(kc + 3)
        stage2(kc)
        stage3(kc)
        xg[...] = jnp.dot(pick[...], x_all[kc], preferred_element_type=F32).astype(BF16).reshape(local_e, capacity, kc_n)

        @pl.loop(0, local_e)
        def _(e):
            win_copy(e, kc).wait()
            slot = (kc % IN_DEPTH) * local_e + e
            up = jnp.dot(xg[e], win_buf[slot], preferred_element_type=F32)
            if kc > 0:
                up = up + acc[e]
            if kc + 1 < IN_BLOCKS:
                acc[e] = up
            else:
                hid[e] = jax.nn.gelu(up).astype(BF16)
            if kc + IN_DEPTH < IN_BLOCKS:
                win_copy(e, kc + IN_DEPTH).start()

    for kc in range(IN_BLOCKS):
        for kind in range(9):
            d_sent(kind, kc).wait_send()
    for d in range(1, n):
        for c in meta_copies(d):
            c.wait_send()

    def rcopy(kind, oc, src, dst, to):
        return pltpu.make_async_remote_copy(
            src_ref=src, dst_ref=dst, send_sem=r_ssem.at[kind, oc], recv_sem=r_rsem.at[kind, oc],
            device_id={AXIS: to}, device_id_type=MESH)

    def r_copy(kind, oc):
        if kind == PART:
            return rcopy(kind, oc, part_send.at[lax.rem(oc, 2)], part_recv.at[oc], buddy)
        if kind == FAR_R:
            return rcopy(kind, oc, total.at[oc, c_far, 0], far_recv.at[oc, 0], right)
        if kind == FAR_L:
            return rcopy(kind, oc, total.at[oc, c_far, 1], far_recv.at[oc, 1], left)
        if kind == NEAR_R:
            return rcopy(kind, oc, total.at[oc, c_right, 1], fin_recv.at[oc, 0, 1], right)
        if kind == NEAR_L:
            return rcopy(kind, oc, total.at[oc, c_left, 0], fin_recv.at[oc, 1, 0], left)
        if kind == MIX_R:
            return rcopy(kind, oc, total.at[oc, c_right, 0], fin_recv.at[oc, 0, 0], right)
        return rcopy(kind, oc, total.at[oc, c_left, 1], fin_recv.at[oc, 1, 1], left)

    rows = chips * tokens
    half = OUT_COLS // 2
    step_rows = rows // 2

    def partial(rail, dst):
        @pl.loop(0, rows // step_rows)
        def _(i):
            at = pl.multiple_of(rail * rows + i * step_rows, step_rows)
            val = jnp.dot(mix[0, pl.ds(at, step_rows), :], obuf[...], preferred_element_type=F32)
            val += jnp.dot(mix[1, pl.ds(at, step_rows), :], obuf[...], preferred_element_type=F32)
            val += jnp.dot(mix[2, pl.ds(at, step_rows), :], obuf[...], preferred_element_type=F32)
            for t in range(step_rows // tokens):
                for h in range(2):
                    dst[i * (step_rows // tokens) + t, h] = val[
                        t * tokens:(t + 1) * tokens, h * half:(h + 1) * half]

    def out_copy(oc):
        return pltpu.make_async_copy(
            out_buf.at[oc], out_hbm.at[:, pl.ds(oc * OUT_COLS, OUT_COLS)], out_sem.at[oc])

    def finish_far(oc):
        r_copy(FAR_R, oc).wait_recv()
        total[oc, c_right, 0] = total[oc, c_right, 0] + far_recv[oc, 0]
        r_copy(MIX_R, oc).start()
        r_copy(FAR_L, oc).wait_recv()
        total[oc, c_left, 1] = total[oc, c_left, 1] + far_recv[oc, 1]
        r_copy(MIX_L, oc).start()

    per_in = kc_n // OUT_COLS

    def finish(oc):
        for kind in (NEAR_R, NEAR_L, MIX_R, MIX_L):
            r_copy(kind, oc).wait_recv()
        for h in range(2):
            at = pl.multiple_of(lax.rem(oc, per_in) * OUT_COLS + h * half, half)
            x_own = x_all[oc // per_in, pl.ds(pl.multiple_of(me * tokens, tokens), tokens), pl.ds(at, half)]
            val = total[oc, chip, h] + fin_recv[oc, 0, h] + fin_recv[oc, 1, h]
            out_buf[oc, :, h * half:(h + 1) * half] = (x_own.astype(F32) + val).astype(BF16)
        out_copy(oc).start()

    @pl.loop(0, oc_n)
    def _(oc):
        @pl.loop(0, local_e)
        def _(e):
            wout_copy(e, oc).wait()
            slot = lax.rem(oc, OUT_DEPTH) * local_e + e
            val = jnp.dot(hid[e], wout_buf[slot], preferred_element_type=F32)
            obuf[pl.ds(pl.multiple_of(e * capacity, capacity), capacity), :] = val.astype(BF16)

            @pl.when(oc + OUT_DEPTH < oc_n)
            def _():
                wout_copy(e, oc + OUT_DEPTH).start()

        @pl.when(oc >= 2)
        def _():
            r_copy(PART, oc - 2).wait_send()

        partial(other, part_send.at[lax.rem(oc, 2)])
        r_copy(PART, oc).start()
        partial(core, total.at[oc])
        r_copy(PART, oc).wait_recv()
        total[oc] = total[oc] + part_recv[oc]
        for kind in (FAR_R, FAR_L, NEAR_R, NEAR_L):
            r_copy(kind, oc).start()

        @pl.when(oc >= 1)
        def _():
            finish_far(oc - 1)

        @pl.when(oc >= 2)
        def _():
            finish(oc - 2)

    finish_far(oc_n - 1)
    finish(oc_n - 2)
    finish(oc_n - 1)

    for oc in range(oc_n):
        out_copy(oc).wait()
        for kind in range(7):
            if kind != PART or oc >= oc_n - 2:
                r_copy(kind, oc).wait_send()


def solution(mesh):
    n = mesh.shape[AXIS]
    row_spec = P(("data", AXIS), None)
    weight_spec = P(AXIS, None, None)

    def device_step(token_rows, expert_ids, gate_weights, w_in, w_out):
        tokens, top_k = expert_ids.shape
        local_e, model, hidden = w_in.shape
        capacity = n * tokens * top_k // (n * local_e)
        slots = local_e * capacity
        chips = n // 2
        kc_n = model // IN_BLOCKS
        oc_n = model // OUT_COLS
        half = OUT_COLS // 2
        vmem = pl.BlockSpec(memory_space=pltpu.VMEM)
        hbm = pl.BlockSpec(memory_space=pl.ANY)
        dma = pltpu.SemaphoreType.DMA
        return pl.pallas_call(
            functools.partial(body, n, capacity),
            out_shape=jax.ShapeDtypeStruct((tokens, model), BF16),
            in_specs=[vmem, vmem, hbm, hbm, hbm],
            out_specs=hbm,
            scratch_shapes=[
                pltpu.VMEM((n, top_k, tokens), jnp.int32),
                pltpu.VMEM((n, top_k, tokens), F32),
                pltpu.VMEM((IN_BLOCKS, n * tokens, kc_n), BF16),
                pltpu.VMEM((slots, n * tokens), BF16),
                pltpu.VMEM((n, 4 * local_e, tokens), F32),
                pltpu.VMEM((3, n * tokens, slots), BF16),
                pltpu.VMEM((local_e, capacity, kc_n), BF16),
                pltpu.VMEM((local_e, capacity, hidden), F32),
                pltpu.VMEM((local_e, capacity, hidden), BF16),
                pltpu.VMEM((slots, OUT_COLS), BF16),
                pltpu.VMEM((2, chips, 2, tokens, half), F32),
                pltpu.VMEM((oc_n, chips, 2, tokens, half), F32),
                pltpu.VMEM((oc_n, chips, 2, tokens, half), F32),
                pltpu.VMEM((oc_n, 2, tokens, half), F32),
                pltpu.VMEM((oc_n, 2, 2, tokens, half), F32),
                pltpu.VMEM((oc_n, tokens, OUT_COLS), BF16),
                pltpu.VMEM((IN_DEPTH * local_e, kc_n, hidden), BF16),
                pltpu.VMEM((OUT_DEPTH * local_e, hidden, OUT_COLS), BF16),
                dma((2, n)), dma((2, n)),
                dma((9, IN_BLOCKS)), dma((9, IN_BLOCKS)),
                dma((7, oc_n)), dma((7, oc_n)),
                dma((IN_BLOCKS,)),
                dma((IN_DEPTH * local_e,)),
                dma((OUT_DEPTH * local_e,)),
                dma((oc_n,)),
            ],
            compiler_params=pltpu.CompilerParams(
                collective_id=0, has_side_effects=True, vmem_limit_bytes=67043328),
        )(expert_ids.T, gate_weights.T, token_rows, w_in, w_out)

    return jax.shard_map(device_step, mesh=mesh, in_specs=(row_spec, row_spec, row_spec, weight_spec, weight_spec),
                         out_specs=row_spec, check_vma=False)
```

time: 288 us -> 95.9 us (0.33)
  Pallas kernels: 0 us -> 93.5 us
  blocking collectives: 86 us -> 0 us
  waiting for transfers between devices: 73.2 us -> 0 us
  local copies, waits for them, and re-layouts: 53.3 us -> 1.88 us
  matrix products: 48.9 us -> 0 us
  starting transfers between devices: 15.6 us -> 0 us
  other arithmetic: 9.38 us -> 0 us
    pallas_call x0 -> x1, Pallas kernels: none -> 93.5 us  [device_step(): pl.pallas_call(functools.partial(body, n, capacity), out_shape=jax.ShapeD...]
    all_to_all x1 -> x0, blocking collectives: 77.1 us -> none  [device_step(): lax.all_to_all(outbound, 'expert', 0, 0, tiled=True)]
    all_to_all x1 -> x0, waiting for transfers between devices: 71.9 us -> none  [device_step(): lax.all_to_all(expert_out.reshape(experts, send_cap, model_dim), 'expert'...]
    dot_general x2 -> x0, matrix products: 48.9 us -> none  [the longest x1 30 us: device_step(): jnp.einsum('gesd,edf->gesf', inbound, w_in, preferred_element_type=jnp.fl...]
    gather x5 -> x0, local copies, waits for them, and re-layouts: 31.6 us -> none  [the longest x2 15 us: device_step(): jnp.take(padded, source_row, axis=0).reshape(experts, send_cap, model_dim)]
    reshape x3 -> x0, local copies, waits for them, and re-layouts: 13.9 us -> none  [the longest x1 8.16 us: device_step(): lax.all_to_all(expert_out.reshape(experts, send_cap, model_dim), 'expert'...]
    ppermute x3 -> x0, starting transfers between devices: 10.7 us -> none  [device_step(): inclusive = inclusive + lax.ppermute(inclusive, 'expert', pairs_list)]
    psum x1 -> x0, blocking collectives: 8.92 us -> none  [device_step(): totals = lax.psum(counts, 'expert')]
  transfers between devices with their start and end apart: 4 -> 0, of which waited for: 2 -> 0; matrix products, arithmetic and copies ran while one was open for 2% -> 0% of each run, Pallas kernels for 0% -> 0%
where the time goes in v1:
time: 95.9 us; the launch traced here: 95.4 us
  Pallas kernels  93.5 us (97%)
  local copies, waits for them, and re-layouts  1.88 us (2%)
    pallas_call x1, Pallas kernels, device_step(): pl.pallas_call(functools.partial(body, n, capacity), out_shape=jax.ShapeD...  93.5 us

profile of v1, /device:TPU:112, one launch (start us, length us, event | category | flops | bytes accessed | tf_op | source)
XLA Modules:
  0.0 95.4 jit_solution(13855188560586797201)
XLA Ops:
  0.0 93.5 %shard_map.55 = bf16[128,2048]{1,0:T(8,128)(2,1)} custom-call(s32[6,128]{1,0:T(8,128)} %bitcast.2, f32[6,128]{1,0:T(8,128)} %bitcast.3, bf16[128,2048]{1,0:T(8,128)(2,1)} %x_hbm.1, bf16[8,2048,1408]{2,1,0:T(8,128)(2,1)} %w_in.1, bf16[8,1408,2048]{2,1,0:T(8,128)(2,1)} %w_out.1), custom_call_target="tpu_custom_call" | custom-call | tf_op jit(solution)/shard_map/pallas_call | solution.py:404
  93.5 1.9 %copy.7 = bf16[128,2048]{1,0:T(8,128)(2,1)} copy(bf16[128,2048]{1,0:T(8,128)(2,1)} %shard_map.55) | data formatting | bytes 1048576
